TPU v7x, 32 devices: a whole 2x2x4 slice. The times are simulated.
32 devices in a mesh: expert: 8 (over z, x), dp: 4 (over y, core).
Axes of the slice: x: 2, y: 2, z: 4, core: 2. Of those that a mesh axis runs over, the one named last changes fastest.
Arguments:
- tokens: bfloat16 [8192, 2048], P(('expert', 'dp')), may hold values from -256 to 256
- routes: int32 [8192, 2], P(('expert', 'dp')), may hold values from 0 to 31, all different within a row
- priority: int32 [32, 256], P(('expert', 'dp')), may hold values from 0 to 255, each once within a row
- router: bfloat16 [2048, 32], replicated, may hold values from -3 to 3
- w_in: bfloat16 [32, 2048, 1024], P(('expert', 'dp')), may hold values from -0.125 to 0.125
- w_out: bfloat16 [32, 2048, 1024], P(('expert', 'dp')), may hold values from -0.1875 to 0.1875
Outputs:
- mixed: bfloat16 [8192, 2048], P(('expert', 'dp'))
- aux_loss: float32 [], replicated
Inputs may be any that keep to these rules, and one draw needn't show every extreme that they name: `routes`: a token's two experts differ; every expert is named by some token. `priority`: each group's 256 tokens hold every rank once.
All inputs are finite; a program needn't handle non-finite values.
Results may differ from a plain program's by a relative error of at most 0.0014.
The roundings to bfloat16 on the way count: a program that leaves them out, or rounds other values in their place, can miss the bound.
Values may be sent and summed in bfloat16 or wider, within the bound.
A program may use at most 64 MiB of HBM per device.

v0:
```python
import jax
import jax.numpy as jnp
from jax import lax
from jax.sharding import PartitionSpec as P


def send_rows(outgoing):
    column = lax.all_to_all(outgoing, "dp", split_axis=1, concat_axis=1, tiled=True)
    arrived = lax.all_to_all(column, "expert", split_axis=0, concat_axis=0, tiled=True)
    return arrived


def return_rows(produced):
    column = lax.all_to_all(produced, "expert", split_axis=0, concat_axis=0, tiled=True)
    returned = lax.all_to_all(column, "dp", split_axis=1, concat_axis=1, tiled=True)
    return returned


def shards(tokens, routes, priority, router, w_in, w_out):
    group_rows = tokens.shape[0]
    width = tokens.shape[1]
    experts = router.shape[1]
    slot_cap = 4 * group_rows // experts
    owner_count = lax.axis_size("expert")
    column_count = lax.axis_size("dp")
    logits = jnp.dot(tokens, router, preferred_element_type=jnp.float32)
    probs = jax.nn.softmax(logits, axis=-1)
    expert_grid = lax.broadcasted_iota(jnp.int32, (group_rows, experts), 1)
    first = routes[:, 0]
    second = routes[:, 1]
    first_hot = (expert_grid == first[:, None]).astype(jnp.float32)
    second_hot = (expert_grid == second[:, None]).astype(jnp.float32)
    logit_first = jnp.sum(logits * first_hot, axis=1)
    logit_second = jnp.sum(logits * second_hot, axis=1)
    gate_first = jax.nn.sigmoid(logit_first - logit_second).astype(jnp.bfloat16)
    gate_second = jax.nn.sigmoid(logit_second - logit_first).astype(jnp.bfloat16)
    ranks = priority[0]
    earlier = (ranks[None, :] < ranks[:, None]).astype(jnp.bfloat16)
    before_first = jnp.dot(
        earlier, first_hot.astype(jnp.bfloat16), preferred_element_type=jnp.float32
    )
    before_second = jnp.dot(
        earlier, second_hot.astype(jnp.bfloat16), preferred_element_type=jnp.float32
    )
    first_load = jnp.sum(first_hot, axis=0)
    pos_first = jnp.sum(before_first * first_hot, axis=1).astype(jnp.int32)
    pos_second = jnp.sum((before_second + first_load[None, :]) * second_hot, axis=1).astype(
        jnp.int32
    )
    slot_first = jnp.where(pos_first < slot_cap, first * slot_cap + pos_first, -1)
    slot_second = jnp.where(pos_second < slot_cap, second * slot_cap + pos_second, -1)
    slot_grid = lax.broadcasted_iota(jnp.int32, (experts * slot_cap, group_rows), 0)
    dispatch = ((slot_grid == slot_first[None, :]) | (slot_grid == slot_second[None, :])).astype(
        jnp.bfloat16
    )
    outgoing = jnp.dot(dispatch, tokens, preferred_element_type=jnp.float32).astype(jnp.bfloat16)
    outgoing = outgoing.reshape(owner_count, column_count, slot_cap, width)
    arrived = send_rows(outgoing)
    expert_rows = arrived.reshape(experts * slot_cap, width)
    hidden = jax.nn.relu(jnp.dot(expert_rows, w_in[0], preferred_element_type=jnp.float32)).astype(
        jnp.bfloat16
    )
    produced = lax.dot_general(
        hidden, w_out[0], (((1,), (1,)), ((), ())), preferred_element_type=jnp.float32
    ).astype(jnp.bfloat16)
    returned = return_rows(produced.reshape(owner_count, column_count, slot_cap, width))
    returned = returned.reshape(experts * slot_cap, width)
    token_grid = lax.broadcasted_iota(jnp.int32, (group_rows, experts * slot_cap), 1)
    nothing = jnp.zeros((), jnp.bfloat16)
    combine = jnp.where(
        token_grid == slot_first[:, None], gate_first[:, None], nothing
    ) + jnp.where(token_grid == slot_second[:, None], gate_second[:, None], nothing)
    mixed = jnp.dot(combine, returned, preferred_element_type=jnp.float32).astype(jnp.bfloat16)
    prob_sum = jnp.sum(probs, axis=0)
    statistics = jnp.stack([prob_sum, first_load], axis=0)
    all_tokens = group_rows * owner_count * column_count
    totals = lax.psum(statistics, ("expert", "dp"))
    aux_loss = experts * jnp.sum(totals[0] / all_tokens * (totals[1] / all_tokens))
    return (mixed, aux_loss)


def solution(mesh):
    placed = (
        P(("expert", "dp"), None),
        P(("expert", "dp"), None),
        P(("expert", "dp"), None),
        P(),
        P(("expert", "dp"), None, None),
        P(("expert", "dp"), None, None),
    )
    return jax.shard_map(
        shards,
        mesh=mesh,
        in_specs=placed,
        out_specs=(P(("expert", "dp"), None), P()),
        check_vma=False,
    )
```

profile of v0, /device:TPU:6, one launch (start us, length us, event | category | flops | bytes accessed | tf_op | source)
XLA Modules:
  0.0 357.8 jit_solution(15551242178874864396)
XLA Ops:
  0.6 0.0 copy-start
  0.6 0.8 fusion.38
  1.4 1.0 fusion.10
  2.5 0.0 copy-done
  2.5 1.3 fusion.39
  3.8 0.1 divide_reduce_fusion
  4.0 1.0 fusion.11
  5.0 1.3 convolution_convert_fusion
  6.3 0.6 copy.14
  6.9 49.6 %all_to_all.20 = bf16[8,4,32,2048]{3,2,0,1:T(8,128)(2,1)S(1)} all-to-all(bf16[8,4,32,2048]{3,2,0,1:T(8,128)(2,1)S(1)} %copy.14), channel_id=1, replica_groups=mesh['expert'=8,'dp'=4] {'dp'}, dimensions={1} | all-to-all | bytes 8388608 | tf_op jit(solution)/shard_map/all_to_all | solution.py:8
  56.5 0.6 copy.15
  57.1 0.0 copy-start.2
  57.1 99.1 %all_to_all.21 = bf16[8,4,32,2048]{3,2,1,0:T(8,128)(2,1)S(1)} all-to-all(bf16[8,4,32,2048]{3,2,1,0:T(8,128)(2,1)S(1)} %copy.15), channel_id=1, replica_groups=mesh['expert'=8,'dp'=4] {'expert'}, dimensions={0} | all-to-all | bytes 8388608 | tf_op jit(solution)/shard_map/all_to_all | solution.py:9
  156.1 0.0 copy-done.2
  156.2 0.0 copy-start.3
  156.2 4.7 %maximum_convert_fusion = bf16[1024,1024]{1,0:T(8,128)(2,1)S(1)} fusion(bf16[1024,2048]{1,0:T(8,128)(2,1)S(1)} %bitcast.31, bf16[1,2048,1024]{2,1,0:T(8,128)(2,1)S(1)} %copy-done.2), kind=kOutput, calls=%fused_computation.4 | convolution fusion | flops 4297064448 | bytes 10485760 | tf_op jit(solution)/shard_map/dot_general | solution.py:60
  160.9 0.0 copy-done.3
  160.9 4.8 %fusion.4 = bf16[1024,2048]{1,0:T(8,128)(2,1)S(1)} fusion(bf16[1024,1024]{1,0:T(8,128)(2,1)S(1)} %maximum_convert_fusion, bf16[1,2048,1024]{2,1,0:T(8,128)(2,1)S(1)} %copy-done.3), kind=kOutput, calls=%fused_computation.6 | convolution fusion | flops 4297064448 | bytes 10485760 | tf_op jit(solution)/shard_map/dot_general | solution.py:63
  165.7 96.3 %all_to_all.22 = bf16[8,4,32,2048]{3,2,1,0:T(8,128)(2,1)S(1)} all-to-all(bf16[8,4,32,2048]{3,2,1,0:T(8,128)(2,1)S(1)} %bitcast.32), channel_id=1, replica_groups=mesh['expert'=8,'dp'=4] {'expert'}, dimensions={0} | all-to-all | bytes 8388608 | tf_op jit(solution)/shard_map/all_to_all | solution.py:14
  261.9 2.3 copy.16
  264.2 0.0 copy-start.1
  264.2 6.0 %all-to-all-start.3 = ((bf16[8,4,32,2048]{3,2,0,1:T(8,128)(2,1)}), bf16[8,4,32,2048]{3,2,0,1:T(8,128)(2,1)}, u32[]{:S(2)}, u32[]{:S(2)}) async-start(bf16[8,4,32,2048]{3,2,0,1:T(8,128)(2,1)} %copy.16), calls=%async_computation.3 | async-start | bytes 8388608 | tf_op jit(solution)/shard_map/all_to_all | solution.py:15
  270.3 80.1 %psum.7 = f32[2,32]{1,0:T(2,128)S(1)} all-reduce(f32[2,32]{1,0:T(2,128)S(1)} %pad_maximum_fusion), channel_id=1, replica_groups=mesh['expert'=8,'dp'=4] {'expert','dp'}, use_global_device_ids=true, to_apply=%region_8.9 | all-reduce | flops 64 | bytes 512 | tf_op jit(solution)/shard_map/psum | solution.py:77
  350.4 0.6 multiply_reduce_fusion
  351.6 0.0 copy-done.1
  351.7 0.0 all-to-all-done.3
  351.7 2.5 copy.17
  354.2 2.4 convolution_convert_fusion.1
  (7 shorter events, 0.1 us)
Async XLA Ops:
  0.6 1.8 copy-start
  57.1 99.1 %copy-start.2 = (bf16[1,2048,1024]{2,1,0:T(8,128)(2,1)S(1)}, bf16[1,2048,1024]{2,1,0:T(8,128)(2,1)}, u32[]{:S(2)}) copy-start(bf16[1,2048,1024]{2,1,0:T(8,128)(2,1)} %param.10) | copy-start | bytes 12582916
  156.2 4.7 %copy-start.3 = (bf16[1,2048,1024]{2,1,0:T(8,128)(2,1)S(1)}, bf16[1,2048,1024]{2,1,0:T(8,128)(2,1)}, u32[]{:S(2)}) copy-start(bf16[1,2048,1024]{2,1,0:T(8,128)(2,1)} %param.11) | copy-start | bytes 12582916
  264.2 87.4 %copy-start.1 = (s32[256,2]{0,1:T(2,128)S(1)}, s32[256,2]{0,1:T(2,128)}, u32[]{:S(2)}) copy-start(s32[256,2]{0,1:T(2,128)} %param.7) | copy-start | bytes 6148
  264.2 87.5 %all-to-all-start.3 = ((bf16[8,4,32,2048]{3,2,0,1:T(8,128)(2,1)}), bf16[8,4,32,2048]{3,2,0,1:T(8,128)(2,1)}, u32[]{:S(2)}, u32[]{:S(2)}) async-start(bf16[8,4,32,2048]{3,2,0,1:T(8,128)(2,1)} %copy.16), calls=%async_computation.3 | async-start | bytes 8388608 | tf_op jit(solution)/shard_map/all_to_all | solution.py:15
where the time goes:
time: 360 us; the launch traced here: 358 us
  blocking collectives  325 us (90%)
  matrix products  16.6 us (5%)
  local copies, waits for them, and re-layouts  6.74 us (2%)
  starting transfers between devices  6.05 us (2%)
    all_to_all x1, blocking collectives, send_rows(): lax.all_to_all(column, 'expert', split_axis=0, concat_axis=0, tiled=True)  99.1 us
    all_to_all x1, blocking collectives, return_rows(): lax.all_to_all(produced, 'expert', split_axis=0, concat_axis=0, tiled=True)  96.3 us
    psum x1, blocking collectives, shards(): totals = lax.psum(statistics, ('expert', 'dp'))  80.1 us
    all_to_all x1, blocking collectives, send_rows(): lax.all_to_all(outgoing, 'dp', split_axis=1, concat_axis=1, tiled=True)  49.6 us
  transfers between devices with their start and end apart: 1, of which 0 were waited for; matrix products, arithmetic and copies ran while one was open for 0% of the time, Pallas kernels for 0%

commit v1 on v0

--- a/solution.py
+++ b/solution.py
@@ -1,7 +1,366 @@
+import functools
+
 import jax
 import jax.numpy as jnp
 from jax import lax
+from jax.experimental import pallas as pl
+from jax.experimental.pallas import tpu as pltpu
 from jax.sharding import PartitionSpec as P
+
+MESH = pl.DeviceIdType.MESH
+LINES = 4
+
+
+def exchange_kernel(
+    lanes,
+    columns,
+    cap,
+    tokens,
+    meta,
+    combine,
+    stats,
+    w_in_hbm,
+    w_out_hbm,
+    mixed,
+    aux,
+    tok_all,
+    meta_all,
+    out,
+    arrived,
+    produced,
+    returned,
+    hidden,
+    total,
+    stats_all,
+    w_in,
+    w_out,
+    weight_sem,
+    tok_send,
+    tok_recv,
+    meta_send,
+    meta_recv,
+    stat_send,
+    stat_recv,
+    out_send,
+    out_recv,
+    ret_send,
+    ret_recv,
+):
+    plane = lanes * columns
+    devices = LINES * plane
+    rows = plane * cap
+    group_rows, width = tokens.shape
+    units = w_in.shape[1]
+    owner = lax.axis_index("expert")
+    column = lax.axis_index("dp")
+    z = owner // lanes
+    p = (owner % lanes) * columns + column
+    me = z * plane + p
+
+    def place(line, spot):
+        return (line * lanes + spot // columns, spot % columns)
+
+    load_in = pltpu.make_async_copy(w_in_hbm.at[0], w_in, weight_sem.at[0])
+    load_out = pltpu.make_async_copy(w_out_hbm.at[0], w_out, weight_sem.at[1])
+    load_in.start()
+    load_out.start()
+
+    barrier = pltpu.get_barrier_semaphore()
+    for shift in range(1, devices):
+        other = (me + shift) % devices
+        pl.semaphore_signal(
+            barrier, inc=1, device_id=place(other // plane, other % plane), device_id_type=MESH
+        )
+    pl.semaphore_wait(barrier, devices - 1)
+
+    def line_copies(group, own, way):
+        line = z + 1 - 2 * way
+        return (
+            pltpu.make_async_remote_copy(
+                src_ref=meta if own else meta_all.at[group],
+                dst_ref=meta_all.at[group],
+                send_sem=meta_send.at[way, group],
+                recv_sem=meta_recv.at[group],
+                device_id=place(line, p),
+                device_id_type=MESH,
+            ),
+            pltpu.make_async_remote_copy(
+                src_ref=tokens if own else tok_all.at[group],
+                dst_ref=tok_all.at[group],
+                send_sem=tok_send.at[way, group],
+                recv_sem=tok_recv.at[group],
+                device_id=place(line, p),
+                device_id_type=MESH,
+            ),
+        )
+
+    def send_line(group, own, way):
+        for copy in line_copies(group, own, way):
+            copy.start()
+
+    def take_line(group):
+        for copy in line_copies(group, False, 0):
+            copy.wait_recv()
+
+    @pl.when(z < LINES - 1)
+    def _():
+        send_line(z, True, 0)
+
+    @pl.when(z > 0)
+    def _():
+        send_line(z, True, 1)
+
+    def stat_copy(shift):
+        other = (me + shift) % devices
+        return pltpu.make_async_remote_copy(
+            src_ref=stats,
+            dst_ref=stats_all.at[shift],
+            send_sem=stat_send.at[shift],
+            recv_sem=stat_recv.at[shift],
+            device_id=place(other // plane, other % plane),
+            device_id_type=MESH,
+        )
+
+    for shift in range(1, devices):
+        stat_copy(shift).start()
+
+    half = z // (LINES // 2)
+    near = z * (1 - half) + (LINES - 1 - z) * half
+    order = []
+    for value in (near, 1 + near, 2 - 2 * near, LINES - 1):
+        order.append(value * (1 - half) + (LINES - 1 - value) * half)
+
+    def hop(distance):
+        @pl.when(z >= distance)
+        def _():
+            take_line(z - distance)
+
+            @pl.when(z < LINES - 1)
+            def _():
+                send_line(z - distance, False, 0)
+
+        @pl.when(z + distance < LINES)
+        def _():
+            take_line(z + distance)
+
+            @pl.when(z > 0)
+            def _():
+                send_line(z + distance, False, 1)
+
+    def out_copy(step, shift):
+        spot = (p + shift) % plane
+        return pltpu.make_async_remote_copy(
+            src_ref=out.at[step, pl.ds(pl.multiple_of(spot * cap, cap), cap)],
+            dst_ref=arrived.at[step, pl.ds(pl.multiple_of(p * cap, cap), cap)],
+            send_sem=out_send.at[step, shift],
+            recv_sem=out_recv.at[step, shift],
+            device_id=place(z, spot),
+            device_id_type=MESH,
+        )
+
+    def own_out(step):
+        mine = pl.ds(pl.multiple_of(p * cap, cap), cap)
+        return pltpu.make_async_copy(
+            out.at[step, mine], arrived.at[step, mine], out_recv.at[step, 0]
+        )
+
+    def dispatch(step):
+        group = order[step]
+        slots = (meta if step == 0 else meta_all.at[group])[...] - z * rows
+        grid = lax.broadcasted_iota(jnp.int32, (rows, group_rows), 0)
+        hot = (grid == slots[0:1, :]) | (grid == slots[1:2, :])
+        hot = jnp.where(hot, 1.0, 0.0).astype(jnp.bfloat16)
+        tile = 512
+
+        def body(j, carry):
+            cols = pl.ds(pl.multiple_of(j * tile, tile), tile)
+            block = tokens[:, cols] if step == 0 else tok_all[group, :, cols]
+            out[step, :, cols] = jnp.dot(
+                hot, block, preferred_element_type=jnp.float32
+            ).astype(jnp.bfloat16)
+            return carry
+
+        lax.fori_loop(0, width // tile, body, 0)
+        own_out(step).start()
+        for shift in range(1, plane):
+            out_copy(step, shift).start()
+
+    def ret_copy(step, shift):
+        spot = (p + shift) % plane
+        return pltpu.make_async_remote_copy(
+            src_ref=produced.at[step, pl.ds(pl.multiple_of(spot * cap, cap), cap)],
+            dst_ref=returned.at[z, pl.ds(pl.multiple_of(p * cap, cap), cap)],
+            send_sem=ret_send.at[step, shift],
+            recv_sem=ret_recv.at[z, shift],
+            device_id=place(order[step], spot),
+            device_id_type=MESH,
+        )
+
+    def own_ret():
+        mine = pl.ds(pl.multiple_of(p * cap, cap), cap)
+        return pltpu.make_async_copy(
+            produced.at[0, mine], returned.at[z, mine], ret_recv.at[z, 0]
+        )
+
+    def run_expert(step):
+        own_out(step).wait()
+        for shift in range(1, plane):
+            out_copy(step, shift).wait_recv()
+        if step == 0:
+            load_in.wait()
+            load_out.wait()
+        tile = 256
+
+        def up(j, carry):
+            cols = pl.ds(pl.multiple_of(j * tile, tile), tile)
+            value = jnp.dot(arrived[step], w_in[:, cols], preferred_element_type=jnp.float32)
+            hidden[:, cols] = jnp.maximum(value, 0.0).astype(jnp.bfloat16)
+            return carry
+
+        lax.fori_loop(0, units // tile, up, 0)
+
+        def down(j, carry):
+            cols = pl.ds(pl.multiple_of(j * tile, tile), tile)
+            value = lax.dot_general(
+                hidden[...],
+                w_out[cols, :],
+                (((1,), (1,)), ((), ())),
+                preferred_element_type=jnp.float32,
+            )
+            produced[step, :, cols] = value.astype(jnp.bfloat16)
+            return carry
+
+        lax.fori_loop(0, width // tile, down, 0)
+        if step == 0:
+            own_ret().start()
+        for shift in range(1 if step == 0 else 0, plane):
+            ret_copy(step, shift).start()
+
+    def gather(step):
+        line = order[step]
+        if step == 0:
+            own_ret().wait()
+        for shift in range(1 if step == 0 else 0, plane):
+            pltpu.make_async_remote_copy(
+                src_ref=produced.at[0, pl.ds(0, cap)],
+                dst_ref=returned.at[line, pl.ds(pl.multiple_of(((p + plane - shift) % plane) * cap, cap), cap)],
+                send_sem=ret_send.at[0, shift],
+                recv_sem=ret_recv.at[line, shift],
+                device_id=place(line, p),
+                device_id_type=MESH,
+            ).wait_recv()
+        tile = 512
+
+        def body(j, carry):
+            cols = pl.ds(pl.multiple_of(j * tile, tile), tile)
+            value = jnp.dot(
+                combine[line], returned[line, :, cols], preferred_element_type=jnp.float32
+            )
+            if step > 0:
+                value = total[:, cols] + value
+            if step < LINES - 1:
+                total[:, cols] = value
+            else:
+                mixed[:, cols] = value.astype(jnp.bfloat16)
+            return carry
+
+        lax.fori_loop(0, width // tile, body, 0)
+
+    dispatch(0)
+    run_expert(0)
+    hop(1)
+    dispatch(1)
+    run_expert(1)
+    hop(2)
+    dispatch(2)
+    run_expert(2)
+    hop(3)
+    dispatch(3)
+    run_expert(3)
+    gather(0)
+
+    sums = stats[...]
+    for shift in range(1, devices):
+        stat_copy(shift).wait()
+        sums = sums + stats_all[shift]
+    everyone = group_rows * devices
+    share = (sums[0:1, :] / everyone) * (sums[1:2, :] / everyone)
+    aux[...] = jnp.broadcast_to(devices * jnp.sum(share, axis=1, keepdims=True), aux.shape)
+
+    gather(1)
+    gather(2)
+    gather(3)
+
+    for way in range(2):
+        moves = (z < LINES - 1) if way == 0 else (z > 0)
+
+        @pl.when(moves)
+        def _():
+            for copy in line_copies(z, True, way):
+                copy.wait_send()
+
+        for distance in range(1, LINES):
+            passes = (z >= distance) if way == 0 else (z + distance < LINES)
+
+            @pl.when(moves & passes)
+            def _():
+                group = z - distance if way == 0 else z + distance
+                for copy in line_copies(group, False, way):
+                    copy.wait_send()
+
+    for step in range(LINES):
+        for shift in range(1, plane):
+            out_copy(step, shift).wait_send()
+        for shift in range(1 if step == 0 else 0, plane):
+            ret_copy(step, shift).wait_send()
+
+
+def exchange(tokens, meta, combine, stats, w_in, w_out, lanes, columns, cap):
+    group_rows, width = tokens.shape
+    units = w_in.shape[2]
+    plane = lanes * columns
+    rows = plane * cap
+    devices = LINES * plane
+    vmem = pl.BlockSpec(memory_space=pltpu.VMEM)
+    anywhere = pl.BlockSpec(memory_space=pl.ANY)
+    dma = pltpu.SemaphoreType.DMA
+    half = jnp.bfloat16
+    return pl.pallas_call(
+        functools.partial(exchange_kernel, lanes, columns, cap),
+        out_shape=(
+            jax.ShapeDtypeStruct((group_rows, width), half),
+            jax.ShapeDtypeStruct((8, 128), jnp.float32),
+        ),
+        in_specs=[vmem, vmem, vmem, vmem, anywhere, anywhere],
+        out_specs=(vmem, vmem),
+        scratch_shapes=[
+            pltpu.VMEM((LINES, group_rows, width), half),
+            pltpu.VMEM((LINES,) + meta.shape, jnp.int32),
+            pltpu.VMEM((LINES, rows, width), half),
+            pltpu.VMEM((LINES, rows, width), half),
+            pltpu.VMEM((LINES, rows, width), half),
+            pltpu.VMEM((LINES, rows, width), half),
+            pltpu.VMEM((rows, units), half),
+            pltpu.VMEM((group_rows, width), jnp.float32),
+            pltpu.VMEM((devices,) + stats.shape, jnp.float32),
+            pltpu.VMEM((width, units), half),
+            pltpu.VMEM((width, units), half),
+            dma((2,)),
+            dma((2, LINES)),
+            dma((LINES,)),
+            dma((2, LINES)),
+            dma((LINES,)),
+            dma((devices,)),
+            dma((devices,)),
+            dma((LINES, plane)),
+            dma((LINES, plane)),
+            dma((LINES, plane)),
+            dma((LINES, plane)),
+        ],
+        compiler_params=pltpu.CompilerParams(
+            collective_id=0, has_side_effects=True, vmem_limit_bytes=60 * 1024 * 1024
+        ),
+    )(tokens, meta, combine, stats, w_in, w_out)
 
 
 def send_rows(outgoing):
@@ -49,6 +408,25 @@
     )
     slot_first = jnp.where(pos_first < slot_cap, first * slot_cap + pos_first, -1)
     slot_second = jnp.where(pos_second < slot_cap, second * slot_cap + pos_second, -1)
+    prob_sum = jnp.sum(probs, axis=0)
+    if owner_count % LINES == 0 and slot_cap % 16 == 0:
+        lanes = owner_count // LINES
+        rows = lanes * column_count * slot_cap
+        whole_grid = (LINES, group_rows, rows)
+        seats = lax.broadcasted_iota(jnp.int32, whole_grid, 0) * rows + lax.broadcasted_iota(
+            jnp.int32, whole_grid, 2
+        )
+        nothing = jnp.zeros((), jnp.bfloat16)
+        combine = jnp.where(
+            seats == slot_first[None, :, None], gate_first[None, :, None], nothing
+        ) + jnp.where(seats == slot_second[None, :, None], gate_second[None, :, None], nothing)
+        meta = jnp.pad(jnp.stack([slot_first, slot_second], axis=0), ((0, 6), (0, 0)))
+        statistics = jnp.stack([prob_sum, first_load], axis=0)
+        statistics = jnp.pad(statistics, ((0, 6), (0, -experts % 128)))
+        mixed, aux = exchange(
+            tokens, meta, combine, statistics, w_in, w_out, lanes, column_count, slot_cap
+        )
+        return (mixed, aux[0, 0])
     slot_grid = lax.broadcasted_iota(jnp.int32, (experts * slot_cap, group_rows), 0)
     dispatch = ((slot_grid == slot_first[None, :]) | (slot_grid == slot_second[None, :])).astype(
         jnp.bfloat16
@@ -71,7 +449,6 @@
         token_grid == slot_first[:, None], gate_first[:, None], nothing
     ) + jnp.where(token_grid == slot_second[:, None], gate_second[:, None], nothing)
     mixed = jnp.dot(combine, returned, preferred_element_type=jnp.float32).astype(jnp.bfloat16)
-    prob_sum = jnp.sum(probs, axis=0)
     statistics = jnp.stack([prob_sum, first_load], axis=0)
     all_tokens = group_rows * owner_count * column_count
     totals = lax.psum(statistics, ("expert", "dp"))

time: 360 us -> 191 us (0.53)
  blocking collectives: 325 us -> 0 us
  Pallas kernels: 0 us -> 179 us
  matrix products: 16.6 us -> 3.71 us
  starting transfers between devices: 6.05 us -> 0 us
    all_to_all x3 -> x0, blocking collectives: 245 us -> none  [the longest x1 99.1 us: send_rows(): lax.all_to_all(column, 'expert', split_axis=0, concat_axis=0, tiled=True)]
    pallas_call x0 -> x1, Pallas kernels: none -> 179 us  [exchange(): pl.pallas_call(functools.partial(exchange_kernel, lanes, columns, cap), o...]
    psum x1 -> x0, blocking collectives: 80.1 us -> none  [shards(): totals = lax.psum(statistics, ('expert', 'dp'))]
    dot_general x4 -> x0, matrix products: 13.2 us -> none  [the longest x1 4.79 us: shards(): lax.dot_general(hidden, w_out[0], (((1,), (1,)), ((), ())), preferred_ele...]
    all_to_all x1 -> x0, starting transfers between devices: 6.05 us -> none  [return_rows(): lax.all_to_all(column, 'dp', split_axis=1, concat_axis=1, tiled=True)]
    all_to_all x3 -> x0, local copies, waits for them, and re-layouts: 5.35 us -> none  [the longest x1 2.5 us: return_rows(): lax.all_to_all(column, 'dp', split_axis=1, concat_axis=1, tiled=True)]
  transfers between devices with their start and end apart: 1 -> 0, of which waited for: 0 -> 0; matrix products, arithmetic and copies ran while one was open for 0% -> 0% of each run, Pallas kernels for 0% -> 0%
where the time goes in v1:
time: 191 us
  Pallas kernels  179 us (94%)
  local copies, waits for them, and re-layouts  4.85 us (3%)
  matrix products  3.71 us (2%)
  other arithmetic  2.63 us (1%)
    pallas_call x1, Pallas kernels, exchange(): pl.pallas_call(functools.partial(exchange_kernel, lanes, columns, cap), o...  179 us

profile of v1, /device:TPU:6, one launch (start us, length us, event | category | flops | bytes accessed | tf_op | source)
XLA Modules:
  0.0 191.1 jit_solution(10940337076935606288)
XLA Ops:
  0.6 0.0 copy-start
  0.7 0.8 fusion.19
  1.4 1.0 fusion.1
  2.5 0.0 copy-done
  2.5 1.7 fusion.20
  4.2 0.1 divide_reduce_fusion
  4.3 1.0 fusion.2
  5.4 0.8 compare_select_fusion.1
  6.2 0.6 select_maximum_fusion.stats
  6.8 0.6 pad.8.meta
  7.4 1.1 fusion.7.combine
  8.4 179.1 %shard_map.77 = (bf16[256,2048]{1,0:T(8,128)(2,1)}, f32[8,128]{1,0:T(8,128)}) custom-call(bf16[256,2048]{1,0:T(8,128)(2,1)} %tokens.1, s32[8,256]{1,0:T(8,128)} %pad.8.meta, bf16[4,256,256]{2,1,0:T(8,128)(2,1)} %fusion.7.combine, f32[8,128]{1,0:T(8,128)} %select_maximum_fusion.stats, bf16[1,2048,1024]{2,1,0:T(8,128)(2,1)} %w_in_hbm.1, ...), custom_call_target="tpu_custom_call" | custom-call | tf_op jit(solution)/shard_map/pallas_call | solution.py:328
  187.6 1.2 slice.11
  188.7 2.3 %copy.9 = bf16[256,2048]{1,0:T(8,128)(2,1)} copy(bf16[256,2048]{1,0:T(8,128)(2,1)} %get-tuple-element.22) | data formatting | bytes 2097152
  (7 shorter events, 0.1 us)
Async XLA Ops:
  0.6 1.8 copy-start

commit v2 on v1

--- a/solution.py
+++ b/solution.py
@@ -11,18 +11,73 @@
 LINES = 4
 
 
+def route(tokens, routes, priority, router, meta, gates, stats, cap):
+    experts = router.shape[0]
+    group_rows = tokens.shape[0]
+    logits = lax.dot_general(
+        router[...], tokens[...], (((1,), (1,)), ((), ())), preferred_element_type=jnp.float32
+    )
+    shifted = jnp.exp(logits - jnp.max(logits, axis=0, keepdims=True))
+    probs = shifted / jnp.sum(shifted, axis=0, keepdims=True)
+    grid = lax.broadcasted_iota(jnp.int32, (experts, group_rows), 0)
+    first = routes[0:1, :]
+    second = routes[1:2, :]
+    first_hot = jnp.where(grid == first, 1.0, 0.0)
+    second_hot = jnp.where(grid == second, 1.0, 0.0)
+    margin = jnp.sum(logits * first_hot, axis=0, keepdims=True) - jnp.sum(
+        logits * second_hot, axis=0, keepdims=True
+    )
+    gate_first = (1.0 / (1.0 + jnp.exp(-margin))).astype(jnp.bfloat16).astype(jnp.float32)
+    gate_second = (1.0 / (1.0 + jnp.exp(margin))).astype(jnp.bfloat16).astype(jnp.float32)
+    ranks = jnp.broadcast_to(priority[0:1, :].astype(jnp.float32), (group_rows, group_rows))
+    earlier = jnp.where(jnp.transpose(ranks) < ranks, 1.0, 0.0).astype(jnp.bfloat16)
+    before_first = jnp.dot(
+        first_hot.astype(jnp.bfloat16), earlier, preferred_element_type=jnp.float32
+    )
+    before_second = jnp.dot(
+        second_hot.astype(jnp.bfloat16), earlier, preferred_element_type=jnp.float32
+    )
+    load = jnp.sum(first_hot, axis=1, keepdims=True)
+    pos_first = jnp.sum(before_first * first_hot, axis=0, keepdims=True).astype(jnp.int32)
+    pos_second = jnp.sum((before_second + load) * second_hot, axis=0, keepdims=True).astype(
+        jnp.int32
+    )
+    meta[...] = jnp.full(meta.shape, -1, jnp.int32)
+    meta[0:1, :] = jnp.where(pos_first < cap, first * cap + pos_first, -1)
+    meta[1:2, :] = jnp.where(pos_second < cap, second * cap + pos_second, -1)
+    gates[0:1, :] = gate_first
+    gates[1:2, :] = gate_second
+    ones = jnp.ones((8, group_rows), jnp.float32)
+    sums = []
+    for table in (probs, first_hot):
+        sums.append(
+            lax.dot_general(
+                ones,
+                table,
+                (((1,), (1,)), ((), ())),
+                precision=lax.Precision.HIGHEST,
+                preferred_element_type=jnp.float32,
+            )
+        )
+    row = lax.broadcasted_iota(jnp.int32, sums[0].shape, 0)
+    stats[...] = jnp.where(row == 0, sums[0], sums[1])
+
+
 def exchange_kernel(
     lanes,
     columns,
     cap,
     tokens,
-    meta,
-    combine,
-    stats,
+    routes,
+    priority,
+    router,
     w_in_hbm,
     w_out_hbm,
     mixed,
     aux,
+    meta,
+    gates,
+    stats,
     tok_all,
     meta_all,
     out,
@@ -94,21 +149,26 @@
             ),
         )
 
-    def send_line(group, own, way):
-        for copy in line_copies(group, own, way):
-            copy.start()
+    def send_line(group, own, way, parts=(0, 1)):
+        copies = line_copies(group, own, way)
+        for part in parts:
+            copies[part].start()
 
     def take_line(group):
         for copy in line_copies(group, False, 0):
             copy.wait_recv()
 
-    @pl.when(z < LINES - 1)
-    def _():
-        send_line(z, True, 0)
-
-    @pl.when(z > 0)
-    def _():
-        send_line(z, True, 1)
+    def send_own(parts):
+        @pl.when(z < LINES - 1)
+        def _():
+            send_line(z, True, 0, parts)
+
+        @pl.when(z > 0)
+        def _():
+            send_line(z, True, 1, parts)
+
+    send_own((1,))
+    route(tokens, routes, priority, router, meta, gates, stats, cap)
 
     def stat_copy(shift):
         other = (me + shift) % devices
@@ -121,13 +181,10 @@
             device_id_type=MESH,
         )
 
-    for shift in range(1, devices):
-        stat_copy(shift).start()
-
     half = z // (LINES // 2)
     near = z * (1 - half) + (LINES - 1 - z) * half
     order = []
-    for value in (near, 1 + near, 2 - 2 * near, LINES - 1):
+    for value in (near, 1 + near, 2 + near, 3 - 3 * near):
         order.append(value * (1 - half) + (LINES - 1 - value) * half)
 
     def hop(distance):
@@ -250,11 +307,15 @@
                 device_id_type=MESH,
             ).wait_recv()
         tile = 512
+        grid = lax.broadcasted_iota(jnp.int32, (rows, group_rows), 0) + line * rows
+        weights = jnp.where(grid == meta[0:1, :], gates[0:1, :], 0.0)
+        weights = weights + jnp.where(grid == meta[1:2, :], gates[1:2, :], 0.0)
+        weights = jnp.transpose(weights).astype(jnp.bfloat16)
 
         def body(j, carry):
             cols = pl.ds(pl.multiple_of(j * tile, tile), tile)
             value = jnp.dot(
-                combine[line], returned[line, :, cols], preferred_element_type=jnp.float32
+                weights, returned[line, :, cols], preferred_element_type=jnp.float32
             )
             if step > 0:
                 value = total[:, cols] + value
@@ -267,6 +328,9 @@
         lax.fori_loop(0, width // tile, body, 0)
 
     dispatch(0)
+    send_own((0,))
+    for shift in range(1, devices):
+        stat_copy(shift).start()
     run_expert(0)
     hop(1)
     dispatch(1)
@@ -315,7 +379,7 @@
             ret_copy(step, shift).wait_send()
 
 
-def exchange(tokens, meta, combine, stats, w_in, w_out, lanes, columns, cap):
+def exchange(tokens, routes, priority, router, w_in, w_out, lanes, columns, cap):
     group_rows, width = tokens.shape
     units = w_in.shape[2]
     plane = lanes * columns
@@ -334,15 +398,18 @@
         in_specs=[vmem, vmem, vmem, vmem, anywhere, anywhere],
         out_specs=(vmem, vmem),
         scratch_shapes=[
+            pltpu.VMEM((8, group_rows), jnp.int32),
+            pltpu.VMEM((8, group_rows), jnp.float32),
+            pltpu.VMEM((8, router.shape[0]), jnp.float32),
             pltpu.VMEM((LINES, group_rows, width), half),
-            pltpu.VMEM((LINES,) + meta.shape, jnp.int32),
+            pltpu.VMEM((LINES, 8, group_rows), jnp.int32),
             pltpu.VMEM((LINES, rows, width), half),
             pltpu.VMEM((LINES, rows, width), half),
             pltpu.VMEM((LINES, rows, width), half),
             pltpu.VMEM((LINES, rows, width), half),
             pltpu.VMEM((rows, units), half),
             pltpu.VMEM((group_rows, width), jnp.float32),
-            pltpu.VMEM((devices,) + stats.shape, jnp.float32),
+            pltpu.VMEM((devices, 8, router.shape[0]), jnp.float32),
             pltpu.VMEM((width, units), half),
             pltpu.VMEM((width, units), half),
             dma((2,)),
@@ -360,7 +427,7 @@
         compiler_params=pltpu.CompilerParams(
             collective_id=0, has_side_effects=True, vmem_limit_bytes=60 * 1024 * 1024
         ),
-    )(tokens, meta, combine, stats, w_in, w_out)
+    )(tokens, routes, priority, router, w_in, w_out)
 
 
 def send_rows(outgoing):
@@ -382,6 +449,12 @@
     slot_cap = 4 * group_rows // experts
     owner_count = lax.axis_size("expert")
     column_count = lax.axis_size("dp")
+    if owner_count % LINES == 0 and slot_cap % 16 == 0:
+        lanes = owner_count // LINES
+        mixed, aux = exchange(
+            tokens, routes.T, priority, router.T, w_in, w_out, lanes, column_count, slot_cap
+        )
+        return (mixed, aux[0, 0])
     logits = jnp.dot(tokens, router, preferred_element_type=jnp.float32)
     probs = jax.nn.softmax(logits, axis=-1)
     expert_grid = lax.broadcasted_iota(jnp.int32, (group_rows, experts), 1)
@@ -408,25 +481,6 @@
     )
     slot_first = jnp.where(pos_first < slot_cap, first * slot_cap + pos_first, -1)
     slot_second = jnp.where(pos_second < slot_cap, second * slot_cap + pos_second, -1)
-    prob_sum = jnp.sum(probs, axis=0)
-    if owner_count % LINES == 0 and slot_cap % 16 == 0:
-        lanes = owner_count // LINES
-        rows = lanes * column_count * slot_cap
-        whole_grid = (LINES, group_rows, rows)
-        seats = lax.broadcasted_iota(jnp.int32, whole_grid, 0) * rows + lax.broadcasted_iota(
-            jnp.int32, whole_grid, 2
-        )
-        nothing = jnp.zeros((), jnp.bfloat16)
-        combine = jnp.where(
-            seats == slot_first[None, :, None], gate_first[None, :, None], nothing
-        ) + jnp.where(seats == slot_second[None, :, None], gate_second[None, :, None], nothing)
-        meta = jnp.pad(jnp.stack([slot_first, slot_second], axis=0), ((0, 6), (0, 0)))
-        statistics = jnp.stack([prob_sum, first_load], axis=0)
-        statistics = jnp.pad(statistics, ((0, 6), (0, -experts % 128)))
-        mixed, aux = exchange(
-            tokens, meta, combine, statistics, w_in, w_out, lanes, column_count, slot_cap
-        )
-        return (mixed, aux[0, 0])
     slot_grid = lax.broadcasted_iota(jnp.int32, (experts * slot_cap, group_rows), 0)
     dispatch = ((slot_grid == slot_first[None, :]) | (slot_grid == slot_second[None, :])).astype(
         jnp.bfloat16
@@ -449,6 +503,7 @@
         token_grid == slot_first[:, None], gate_first[:, None], nothing
     ) + jnp.where(token_grid == slot_second[:, None], gate_second[:, None], nothing)
     mixed = jnp.dot(combine, returned, preferred_element_type=jnp.float32).astype(jnp.bfloat16)
+    prob_sum = jnp.sum(probs, axis=0)
     statistics = jnp.stack([prob_sum, first_load], axis=0)
     all_tokens = group_rows * owner_count * column_count
     totals = lax.psum(statistics, ("expert", "dp"))

time: 191 us -> 196 us (1.026); the launches traced: 191 us -> 193 us
  Pallas kernels: 179 us -> 189 us
  matrix products: 3.71 us -> 0 us
  other arithmetic: 2.63 us -> 0 us
    pallas_call x1, Pallas kernels: 179 us -> 189 us  [exchange(): pl.pallas_call(functools.partial(exchange_kernel, lanes, columns, cap), o...]
    dot_general x3 -> x0, matrix products: 3.71 us -> none  [the longest x1 1.66 us: shards(): logits = jnp.dot(tokens, router, preferred_element_type=jnp.float32)]
where the time goes in v2:
time: 196 us; the launch traced here: 193 us
  Pallas kernels  189 us (96%)
  local copies, waits for them, and re-layouts  3.49 us (2%)
    pallas_call x1, Pallas kernels, exchange(): pl.pallas_call(functools.partial(exchange_kernel, lanes, columns, cap), o...  189 us

profile of v2, /device:TPU:6, one launch (start us, length us, event | category | flops | bytes accessed | tf_op | source)
XLA Modules:
  0.0 192.7 jit_solution(12941782186057999056)
XLA Ops:
  0.6 188.6 %shard_map.77 = (bf16[256,2048]{1,0:T(8,128)(2,1)}, f32[8,128]{1,0:T(8,128)}) custom-call(bf16[256,2048]{1,0:T(8,128)(2,1)} %tokens.1, s32[2,256]{1,0:T(2,128)} %bitcast.4, s32[1,256]{1,0:T(1,128)} %priority.1, bf16[32,2048]{1,0:T(8,128)(2,1)} %bitcast.3, bf16[1,2048,1024]{2,1,0:T(8,128)(2,1)} %w_in_hbm.1, bf16[1,2048,1024]{2,1,0:T(8,128)(2,1)} %w_out_hbm.1), custom_call_target="tpu_custom_call" | custom-call | tf_op jit(solution)/shard_map/pallas_call | solution.py:392
  189.2 1.2 slice.3
  190.4 2.3 %copy.9 = bf16[256,2048]{1,0:T(8,128)(2,1)} copy(bf16[256,2048]{1,0:T(8,128)(2,1)} %get-tuple-element.8) | data formatting | bytes 2097152

commit v3 on v2

--- a/solution.py
+++ b/solution.py
@@ -184,7 +184,7 @@
     half = z // (LINES // 2)
     near = z * (1 - half) + (LINES - 1 - z) * half
     order = []
-    for value in (near, 1 + near, 2 + near, 3 - 3 * near):
+    for value in (near, 1 + near, 2 - 2 * near, LINES - 1):
         order.append(value * (1 - half) + (LINES - 1 - value) * half)
 
     def hop(distance):

time: 196 us -> 183 us (0.934); the launches traced: 193 us -> 183 us
  Pallas kernels: 189 us -> 178 us
    pallas_call x1, Pallas kernels: 189 us -> 178 us  [exchange(): pl.pallas_call(functools.partial(exchange_kernel, lanes, columns, cap), o...]
where the time goes in v3:
time: 183 us
  Pallas kernels  178 us (97%)
  local copies, waits for them, and re-layouts  3.49 us (2%)
    pallas_call x1, Pallas kernels, exchange(): pl.pallas_call(functools.partial(exchange_kernel, lanes, columns, cap), o...  178 us

profile of v3, /device:TPU:6, one launch (start us, length us, event | category | flops | bytes accessed | tf_op | source)
XLA Modules:
  0.0 182.5 jit_solution(14359017603278634945)
XLA Ops:
  0.6 178.4 %shard_map.77 = (bf16[256,2048]{1,0:T(8,128)(2,1)}, f32[8,128]{1,0:T(8,128)}) custom-call(bf16[256,2048]{1,0:T(8,128)(2,1)} %tokens.1, s32[2,256]{1,0:T(2,128)} %bitcast.4, s32[1,256]{1,0:T(1,128)} %priority.1, bf16[32,2048]{1,0:T(8,128)(2,1)} %bitcast.3, bf16[1,2048,1024]{2,1,0:T(8,128)(2,1)} %w_in_hbm.1, bf16[1,2048,1024]{2,1,0:T(8,128)(2,1)} %w_out_hbm.1), custom_call_target="tpu_custom_call" | custom-call | tf_op jit(solution)/shard_map/pallas_call | solution.py:392
  179.1 1.2 slice.3
  180.2 2.3 %copy.9 = bf16[256,2048]{1,0:T(8,128)(2,1)} copy(bf16[256,2048]{1,0:T(8,128)(2,1)} %get-tuple-element.8) | data formatting | bytes 2097152
